TPU v7x, 32 devices: a whole 2x2x4 slice. The times are simulated.
32 devices in a mesh: tx: 8 (over z, y), ty: 2 (over x), mem: 2 (over core).
Axes of the slice: x: 2, y: 2, z: 4, core: 2. Of those that a mesh axis runs over, the one named last changes fastest.
Arguments:
- obs_value: float32 [262144], P(('tx', 'ty', 'mem')), may hold values from -6 to 6
- obs_frac: float32 [2, 262144], P(None, ('tx', 'ty', 'mem')), may hold values from 0 to 1
- obs_cell: int32 [262144], P(('tx', 'ty', 'mem')), may hold values from 0 to 2047
- obs_layer: int32 [262144], P(('tx', 'ty', 'mem')), may hold values from 0 to 11
- obs_tile: int32 [262144], P(('tx', 'ty', 'mem')), may hold values from 0 to 15, as said below
- obs_length: int32 [32], P(('tx', 'ty', 'mem')), may hold values from 4096 to 8192, as said below
- ensemble: bfloat16 [80, 6, 2, 128, 256], P('mem', None, None, 'tx', 'ty'), may hold values from -6 to 6
Outputs:
- alpha_grad: bfloat16 [80, 2, 128, 256], P('mem', None, 'tx', 'ty')
Inputs may be any that keep to these rules, and one draw needn't show every extreme that they name: `obs_tile`: among the 8192 entries of one device's list, padding included, at most 1536 name one tile; one tile is named by exactly 1536 live entries of every device's list. `obs_length`: every fourth list is full.
All inputs are finite; a program needn't handle non-finite values.
Results may differ from a plain program's by a relative error of at most 0.001.
Values sent between devices are 32-bit elements; how exact they have to be, the bound alone decides.
A program may use at most 64 MiB of HBM per device.

v0:
```python
import math
import jax
import jax.numpy as jnp
from jax import lax
from jax.sharding import PartitionSpec as P


def shifted(block, axis, distance):
    devices = range(lax.axis_size(axis))
    route = [(i - distance, i) for i in devices if i - distance in devices]
    return lax.ppermute(block, axis, route)


def extended_2(x, sides, width):
    for axis, dim in sides:
        size, length = (lax.axis_size(axis), x.shape[dim])
        up = [(i, (i + 1) % size) for i in range(size - 1)]
        down = [(j, i) for i, j in up]
        last = lax.slice_in_dim(x, length - width, length, axis=dim)
        initial = lax.slice_in_dim(x, 0, width, axis=dim)
        before = lax.ppermute(last, axis, up)
        after = lax.ppermute(initial, axis, down)
        x = jnp.concatenate([before, x, after], axis=dim)
    return x


def smooth(padded):
    along_x = 0.25 * padded[:, :, :-2, :] + 0.5 * padded[:, :, 1:-1, :] + 0.25 * padded[:, :, 2:, :]
    return 0.25 * along_x[:, :, :, :-2] + 0.5 * along_x[:, :, :, 1:-1] + 0.25 * along_x[:, :, :, 2:]


def contract_rows(left, right):
    return lax.dot_general(
        left,
        right,
        (((0,), (0,)), ((), ())),
        precision=lax.Precision.HIGHEST,
        preferred_element_type=jnp.float32,
    )


def body(obs_value, obs_frac, obs_cell, obs_layer, obs_tile, obs_length, ensemble):
    tiles_x = lax.axis_size("tx")
    tiles_y = lax.axis_size("ty")
    tile_count = tiles_x * tiles_y
    row_count = obs_value.shape[0]
    capacity = 3 * row_count // tile_count
    slot_count = ensemble.shape[1]
    level_count = ensemble.shape[2]
    cells_x = ensemble.shape[3]
    cells_y = ensemble.shape[4]
    layer_count = slot_count * level_count
    live_rows = jnp.arange(row_count, dtype=jnp.int32) < obs_length[0]
    one_hot = (
        (obs_tile[:, None] == jnp.arange(tile_count, dtype=jnp.int32)[None, :]) & live_rows[:, None]
    ).astype(jnp.float32)
    blocks = one_hot.reshape(row_count // 128, 128, tile_count)
    lower = jnp.arange(128, dtype=jnp.int32)
    triangle = (lower[:, None] >= lower[None, :]).astype(jnp.float32)
    within = jnp.einsum("ij,bjt->bit", triangle, blocks)
    block_totals = jnp.sum(blocks, axis=1)
    offsets = jnp.cumsum(block_totals, axis=0) - block_totals
    ranking = (
        jnp.sum((within + offsets[:, None, :]) * blocks, axis=-1)
        .reshape(row_count)
        .astype(jnp.int32)
        - 1
    )
    position = obs_layer * (cells_x * cells_y) + obs_cell
    payload = jnp.stack([obs_value, obs_frac[0], obs_frac[1], position.astype(jnp.float32)], axis=1)
    send_block = math.gcd(row_count, 2048)
    slot_ids = jnp.arange(capacity, dtype=jnp.int32)

    def place_rows(step, packed):
        start = step * send_block
        hot = lax.dynamic_slice_in_dim(one_hot, start, send_block, 0)
        load = lax.dynamic_slice_in_dim(payload, start, send_block, 0)
        rank = lax.dynamic_slice_in_dim(ranking, start, send_block, 0)
        slots = (rank[:, None] == slot_ids[None, :]).astype(jnp.float32)
        left = (load[:, :, None] * hot[:, None, :]).reshape(send_block, 4 * tile_count)
        return packed + contract_rows(left, slots)

    packed = lax.fori_loop(
        0, row_count // send_block, place_rows, jnp.zeros((4 * tile_count, capacity), jnp.float32)
    )
    packed = packed.reshape(4, tile_count, capacity)
    send_floats = packed[:3]
    send_index = packed[3:4].astype(jnp.int32)
    got_floats, got_index = (
        lax.all_to_all(send_floats, ("tx", "ty"), split_axis=1, concat_axis=1, tiled=True),
        lax.all_to_all(send_index, ("tx", "ty"), split_axis=1, concat_axis=1, tiled=True),
    )
    got_count = tile_count * capacity
    values = got_floats[0].reshape(-1)
    frac_x = got_floats[1].reshape(-1)
    frac_y = got_floats[2].reshape(-1)
    spot = got_index[0].reshape(-1)
    layer = spot // (cells_x * cells_y)
    column = spot % (cells_x * cells_y)
    column_x = column // cells_y
    column_y = column % cells_y
    recv_block = math.gcd(got_count, 2048)
    layer_ids = jnp.arange(layer_count, dtype=jnp.int32)
    xs_ids = jnp.arange(cells_x + 1, dtype=jnp.int32)
    ys_ids = jnp.arange(cells_y, dtype=jnp.int32)

    def spread_rows(step, carry):
        main, rim = carry
        start = step * recv_block
        val = lax.dynamic_slice_in_dim(values, start, recv_block, 0)
        wfx = lax.dynamic_slice_in_dim(frac_x, start, recv_block, 0)
        wfy = lax.dynamic_slice_in_dim(frac_y, start, recv_block, 0)
        lay = lax.dynamic_slice_in_dim(layer, start, recv_block, 0)
        colx = lax.dynamic_slice_in_dim(column_x, start, recv_block, 0)
        coly = lax.dynamic_slice_in_dim(column_y, start, recv_block, 0)
        layer_hot = jnp.where(lay[:, None] == layer_ids[None, :], val[:, None], jnp.float32(0.0))
        weight_x = jnp.where(colx[:, None] == xs_ids[None, :], 1.0 - wfx[:, None], jnp.float32(0.0))
        weight_x = weight_x + jnp.where(
            colx[:, None] + 1 == xs_ids[None, :], wfx[:, None], jnp.float32(0.0)
        )
        weight_y = jnp.where(coly[:, None] == ys_ids[None, :], 1.0 - wfy[:, None], jnp.float32(0.0))
        weight_y = weight_y + jnp.where(
            coly[:, None] + 1 == ys_ids[None, :], wfy[:, None], jnp.float32(0.0)
        )
        rim_weight = jnp.where(coly + 1 == cells_y, wfy, jnp.float32(0.0))
        left = (layer_hot[:, :, None] * weight_x[:, None, :]).reshape(
            recv_block, layer_count * (cells_x + 1)
        )
        main = main + contract_rows(left, weight_y)
        rim = rim + contract_rows(left, rim_weight)
        return (main, rim)

    start_main = jnp.zeros((layer_count * (cells_x + 1), cells_y), jnp.float32)
    start_rim = jnp.zeros((layer_count * (cells_x + 1),), jnp.float32)
    main, rim = lax.fori_loop(0, got_count // recv_block, spread_rows, (start_main, start_rim))
    extended = main.reshape(layer_count, cells_x + 1, cells_y)
    interior = extended[:, :cells_x, :]
    east_rim = extended[:, cells_x, :]
    north_rim = rim.reshape(layer_count, cells_x + 1)
    from_south = shifted(north_rim, "ty", 1)
    interior = interior.at[:, :, 0].add(from_south[:, :cells_x])
    east_rim = east_rim.at[:, 0].add(from_south[:, cells_x])
    from_west = shifted(east_rim, "tx", 1)
    interior = interior.at[:, 0, :].add(from_west)
    grad = lax.psum(interior, "mem")
    grad_slots = grad.reshape(slot_count, level_count, cells_x, cells_y)
    contrib = jnp.sum(ensemble * grad_slots[None], axis=1)
    padded = extended_2(contrib, (("tx", 2), ("ty", 3)), 1)
    return smooth(padded).astype(jnp.bfloat16)


def solution(mesh):
    placed = (
        P(("tx", "ty", "mem")),
        P(None, ("tx", "ty", "mem")),
        P(("tx", "ty", "mem")),
        P(("tx", "ty", "mem")),
        P(("tx", "ty", "mem")),
        P(("tx", "ty", "mem")),
        P("mem", None, None, "tx", "ty"),
    )
    return jax.shard_map(
        body, mesh=mesh, in_specs=placed, out_specs=P("mem", None, "tx", "ty"), check_vma=False
    )
```

profile of v0, /device:TPU:0, one launch (start us, length us, event | category | flops | bytes accessed | tf_op | source)
XLA Modules:
  0.0 210.7 jit_solution(81586102817702164)
XLA Ops:
  11.5 20.3 %while.34 = (s32[]{:T(128)}, f32[64,1536]{1,0:T(8,128)S(1)}, f32[8192,4]{0,1:T(4,128)S(1)}, f32[8192,16]{0,1:T(8,128)S(1)}, s32[8192]{0:T(1024)S(1)}, /*index=5*/s32[]{:T(128)}, s32[]{:T(128)}, s32[]{:T(128)}, s32[]{:T(128)}) while((s32[]{:T(128)}, f32[64,1536]{1,0:T(8,128)S(1)}, f32[8192,4]{0,1:T(4,128)S(1)}, ...), condition=%wide.region_4.5_spmd.clone, body=%wide.region_3.4_spmd.clone.sunk | while | flops 2419392512 | bytes 2351265 | solution.py:83
  11.7 4.9 %fusion.59 = f32[64,1536]{1,0:T(8,128)S(1)} fusion(f32[2048,64]{0,1:T(8,128)S(1)} %bitcast.59, s32[2048]{0:T(1024)S(1)} %dynamic_slice.94, f32[64,1536]{1,0:T(8,128)S(1)} %get-tuple-element.605, pred[]{:T(512)S(6)} %compare.33), kind=kOutput, calls=%fused_computation.7.clone.1 | convolution fusion | flops 2419261440 | bytes 1318913 | tf_op jit(solution)/shard_map/while/body/eval_jaxpr/dot_general | solution.py:33
  16.7 4.9 %fusion.59 = f32[64,1536]{1,0:T(8,128)S(1)} fusion(f32[2048,64]{0,1:T(8,128)S(1)} %bitcast.59, s32[2048]{0:T(1024)S(1)} %dynamic_slice.94, f32[64,1536]{1,0:T(8,128)S(1)} %get-tuple-element.605, pred[]{:T(512)S(6)} %compare.33), kind=kOutput, calls=%fused_computation.7.clone.1 | convolution fusion | flops 2419261440 | bytes 1318913 | tf_op jit(solution)/shard_map/while/body/eval_jaxpr/dot_general | solution.py:33
  21.8 4.9 %fusion.59 = f32[64,1536]{1,0:T(8,128)S(1)} fusion(f32[2048,64]{0,1:T(8,128)S(1)} %bitcast.59, s32[2048]{0:T(1024)S(1)} %dynamic_slice.94, f32[64,1536]{1,0:T(8,128)S(1)} %get-tuple-element.605, pred[]{:T(512)S(6)} %compare.33), kind=kOutput, calls=%fused_computation.7.clone.1 | convolution fusion | flops 2419261440 | bytes 1318913 | tf_op jit(solution)/shard_map/while/body/eval_jaxpr/dot_general | solution.py:33
  26.9 4.9 %fusion.59 = f32[64,1536]{1,0:T(8,128)S(1)} fusion(f32[2048,64]{0,1:T(8,128)S(1)} %bitcast.59, s32[2048]{0:T(1024)S(1)} %dynamic_slice.94, f32[64,1536]{1,0:T(8,128)S(1)} %get-tuple-element.605, pred[]{:T(512)S(6)} %compare.33), kind=kOutput, calls=%fused_computation.7.clone.1 | convolution fusion | flops 2419261440 | bytes 1318913 | tf_op jit(solution)/shard_map/while/body/eval_jaxpr/dot_general | solution.py:33
  32.6 8.3 %all-to-all-start = ((s32[1,16,1536]{2,0,1:T(1,128)}), s32[1,16,1536]{2,0,1:T(1,128)S(1)}, u32[]{:S(2)}, u32[]{:S(2)}) async-start(s32[1,16,1536]{2,0,1:T(1,128)} %convert_element_type.35), calls=%async_computation | async-start | bytes 196608 | tf_op jit(solution)/shard_map/all_to_all | solution.py:91
  41.9 6.7 %all-to-all-done = s32[1,16,1536]{2,0,1:T(1,128)S(1)} async-done(((s32[1,16,1536]{2,0,1:T(1,128)}), s32[1,16,1536]{2,0,1:T(1,128)S(1)}, u32[]{:S(2)}, u32[]{:S(2)}) %all-to-all-start) | async-done | bytes 98336 | tf_op jit(solution)/shard_map/all_to_all | solution.py:91
  52.4 11.2 %all-to-all-done.1 = f32[3,16,1536]{2,0,1:T(4,128)S(1)} async-done(((f32[3,16,1536]{2,0,1:T(4,128)}), f32[3,16,1536]{2,0,1:T(4,128)S(1)}, u32[]{:S(2)}, u32[]{:S(2)}) %all-to-all-start.1) | async-done | bytes 294944 | tf_op jit(solution)/shard_map/all_to_all | solution.py:90
  63.7 87.0 %while.35 = (s32[]{:T(128)}, f32[204,128]{1,0:T(8,128)S(1)}, f32[204]{0:T(256)S(1)}, s32[24576]{0:T(1024)S(1)}, f32[24576]{0:T(1024)S(1)}, /*index=5*/s32[24576]...) while((s32[]{:T(128)}, f32[204,128]{1,0:T(8,128)S(1)}, ...), condition=%wide.region_6.7_spmd.clone.clone, body=%wide.region_5.6_spmd.clone.clone.sunk | while | flops 648760704 | bytes 15973794 | solution.py:135
  65.6 3.9 %convolution_add_fusion.3 = f32[204,128]{1,0:T(8,128)S(1)} fusion(f32[2048,204]{0,1:T(8,128)} %mul.212, f32[2048]{0:T(1024)S(1)} %get-tuple-element.592, s32[2048]{0:T(1024)S(1)} %broadcast_add_fusion.5, f32[2048]{0:T(1024)S(1)} %broadcast_subtract_fusion.3, s32[2048]{0:T(1024)S(1)} %get-tuple-element.593, f32[204,128]{1,0:T(8,128)S(1)} %get-tuple-element.636, ...), kind=kOutput, calls=%fused_computation.14.clone.1 | convolution fusion | flops 643091456 | bytes 1912833 | tf_op jit(solution)/shard_map/while/body/eval_jaxpr/dot_general | solution.py:33
  72.9 3.9 %convolution_add_fusion.3 = f32[204,128]{1,0:T(8,128)S(1)} fusion(f32[2048,204]{0,1:T(8,128)} %mul.212, f32[2048]{0:T(1024)S(1)} %get-tuple-element.592, s32[2048]{0:T(1024)S(1)} %broadcast_add_fusion.5, f32[2048]{0:T(1024)S(1)} %broadcast_subtract_fusion.3, s32[2048]{0:T(1024)S(1)} %get-tuple-element.593, f32[204,128]{1,0:T(8,128)S(1)} %get-tuple-element.636, ...), kind=kOutput, calls=%fused_computation.14.clone.1 | convolution fusion | flops 643091456 | bytes 1912833 | tf_op jit(solution)/shard_map/while/body/eval_jaxpr/dot_general | solution.py:33
  80.1 3.9 %convolution_add_fusion.3 = f32[204,128]{1,0:T(8,128)S(1)} fusion(f32[2048,204]{0,1:T(8,128)} %mul.212, f32[2048]{0:T(1024)S(1)} %get-tuple-element.592, s32[2048]{0:T(1024)S(1)} %broadcast_add_fusion.5, f32[2048]{0:T(1024)S(1)} %broadcast_subtract_fusion.3, s32[2048]{0:T(1024)S(1)} %get-tuple-element.593, f32[204,128]{1,0:T(8,128)S(1)} %get-tuple-element.636, ...), kind=kOutput, calls=%fused_computation.14.clone.1 | convolution fusion | flops 643091456 | bytes 1912833 | tf_op jit(solution)/shard_map/while/body/eval_jaxpr/dot_general | solution.py:33
  87.4 3.9 %convolution_add_fusion.3 = f32[204,128]{1,0:T(8,128)S(1)} fusion(f32[2048,204]{0,1:T(8,128)} %mul.212, f32[2048]{0:T(1024)S(1)} %get-tuple-element.592, s32[2048]{0:T(1024)S(1)} %broadcast_add_fusion.5, f32[2048]{0:T(1024)S(1)} %broadcast_subtract_fusion.3, s32[2048]{0:T(1024)S(1)} %get-tuple-element.593, f32[204,128]{1,0:T(8,128)S(1)} %get-tuple-element.636, ...), kind=kOutput, calls=%fused_computation.14.clone.1 | convolution fusion | flops 643091456 | bytes 1912833 | tf_op jit(solution)/shard_map/while/body/eval_jaxpr/dot_general | solution.py:33
  94.6 3.9 %convolution_add_fusion.3 = f32[204,128]{1,0:T(8,128)S(1)} fusion(f32[2048,204]{0,1:T(8,128)} %mul.212, f32[2048]{0:T(1024)S(1)} %get-tuple-element.592, s32[2048]{0:T(1024)S(1)} %broadcast_add_fusion.5, f32[2048]{0:T(1024)S(1)} %broadcast_subtract_fusion.3, s32[2048]{0:T(1024)S(1)} %get-tuple-element.593, f32[204,128]{1,0:T(8,128)S(1)} %get-tuple-element.636, ...), kind=kOutput, calls=%fused_computation.14.clone.1 | convolution fusion | flops 643091456 | bytes 1912833 | tf_op jit(solution)/shard_map/while/body/eval_jaxpr/dot_general | solution.py:33
  101.9 3.9 %convolution_add_fusion.3 = f32[204,128]{1,0:T(8,128)S(1)} fusion(f32[2048,204]{0,1:T(8,128)} %mul.212, f32[2048]{0:T(1024)S(1)} %get-tuple-element.592, s32[2048]{0:T(1024)S(1)} %broadcast_add_fusion.5, f32[2048]{0:T(1024)S(1)} %broadcast_subtract_fusion.3, s32[2048]{0:T(1024)S(1)} %get-tuple-element.593, f32[204,128]{1,0:T(8,128)S(1)} %get-tuple-element.636, ...), kind=kOutput, calls=%fused_computation.14.clone.1 | convolution fusion | flops 643091456 | bytes 1912833 | tf_op jit(solution)/shard_map/while/body/eval_jaxpr/dot_general | solution.py:33
  109.1 3.9 %convolution_add_fusion.3 = f32[204,128]{1,0:T(8,128)S(1)} fusion(f32[2048,204]{0,1:T(8,128)} %mul.212, f32[2048]{0:T(1024)S(1)} %get-tuple-element.592, s32[2048]{0:T(1024)S(1)} %broadcast_add_fusion.5, f32[2048]{0:T(1024)S(1)} %broadcast_subtract_fusion.3, s32[2048]{0:T(1024)S(1)} %get-tuple-element.593, f32[204,128]{1,0:T(8,128)S(1)} %get-tuple-element.636, ...), kind=kOutput, calls=%fused_computation.14.clone.1 | convolution fusion | flops 643091456 | bytes 1912833 | tf_op jit(solution)/shard_map/while/body/eval_jaxpr/dot_general | solution.py:33
  116.4 3.9 %convolution_add_fusion.3 = f32[204,128]{1,0:T(8,128)S(1)} fusion(f32[2048,204]{0,1:T(8,128)} %mul.212, f32[2048]{0:T(1024)S(1)} %get-tuple-element.592, s32[2048]{0:T(1024)S(1)} %broadcast_add_fusion.5, f32[2048]{0:T(1024)S(1)} %broadcast_subtract_fusion.3, s32[2048]{0:T(1024)S(1)} %get-tuple-element.593, f32[204,128]{1,0:T(8,128)S(1)} %get-tuple-element.636, ...), kind=kOutput, calls=%fused_computation.14.clone.1 | convolution fusion | flops 643091456 | bytes 1912833 | tf_op jit(solution)/shard_map/while/body/eval_jaxpr/dot_general | solution.py:33
  123.6 3.9 %convolution_add_fusion.3 = f32[204,128]{1,0:T(8,128)S(1)} fusion(f32[2048,204]{0,1:T(8,128)} %mul.212, f32[2048]{0:T(1024)S(1)} %get-tuple-element.592, s32[2048]{0:T(1024)S(1)} %broadcast_add_fusion.5, f32[2048]{0:T(1024)S(1)} %broadcast_subtract_fusion.3, s32[2048]{0:T(1024)S(1)} %get-tuple-element.593, f32[204,128]{1,0:T(8,128)S(1)} %get-tuple-element.636, ...), kind=kOutput, calls=%fused_computation.14.clone.1 | convolution fusion | flops 643091456 | bytes 1912833 | tf_op jit(solution)/shard_map/while/body/eval_jaxpr/dot_general | solution.py:33
  130.9 3.9 %convolution_add_fusion.3 = f32[204,128]{1,0:T(8,128)S(1)} fusion(f32[2048,204]{0,1:T(8,128)} %mul.212, f32[2048]{0:T(1024)S(1)} %get-tuple-element.592, s32[2048]{0:T(1024)S(1)} %broadcast_add_fusion.5, f32[2048]{0:T(1024)S(1)} %broadcast_subtract_fusion.3, s32[2048]{0:T(1024)S(1)} %get-tuple-element.593, f32[204,128]{1,0:T(8,128)S(1)} %get-tuple-element.636, ...), kind=kOutput, calls=%fused_computation.14.clone.1 | convolution fusion | flops 643091456 | bytes 1912833 | tf_op jit(solution)/shard_map/while/body/eval_jaxpr/dot_general | solution.py:33
  138.1 3.9 %convolution_add_fusion.3 = f32[204,128]{1,0:T(8,128)S(1)} fusion(f32[2048,204]{0,1:T(8,128)} %mul.212, f32[2048]{0:T(1024)S(1)} %get-tuple-element.592, s32[2048]{0:T(1024)S(1)} %broadcast_add_fusion.5, f32[2048]{0:T(1024)S(1)} %broadcast_subtract_fusion.3, s32[2048]{0:T(1024)S(1)} %get-tuple-element.593, f32[204,128]{1,0:T(8,128)S(1)} %get-tuple-element.636, ...), kind=kOutput, calls=%fused_computation.14.clone.1 | convolution fusion | flops 643091456 | bytes 1912833 | tf_op jit(solution)/shard_map/while/body/eval_jaxpr/dot_general | solution.py:33
  145.4 3.9 %convolution_add_fusion.3 = f32[204,128]{1,0:T(8,128)S(1)} fusion(f32[2048,204]{0,1:T(8,128)} %mul.212, f32[2048]{0:T(1024)S(1)} %get-tuple-element.592, s32[2048]{0:T(1024)S(1)} %broadcast_add_fusion.5, f32[2048]{0:T(1024)S(1)} %broadcast_subtract_fusion.3, s32[2048]{0:T(1024)S(1)} %get-tuple-element.593, f32[204,128]{1,0:T(8,128)S(1)} %get-tuple-element.636, ...), kind=kOutput, calls=%fused_computation.14.clone.1 | convolution fusion | flops 643091456 | bytes 1912833 | tf_op jit(solution)/shard_map/while/body/eval_jaxpr/dot_general | solution.py:33
  160.4 19.5 %all-reduce.2.cloned.1.call-done = f32[6,2,16,128]{3,2,1,0:T(8,128)} async-done(((f32[6,2,16,128]{3,2,1,0:T(8,128)}), f32[6,2,16,128]{3,2,1,0:T(8,128)}) %all-reduce.2.cloned.1.call-update) | async-done | bytes 98320 | tf_op jit(solution)/shard_map/psum | solution.py:145
  186.7 4.2 %collective-permute-done.3 = f32[40,2,1,128]{3,0,2,1:T(8,128)S(1)} collective-permute-done((f32[40,2,1,128]{3,0,2,1:T(8,128)S(1)}, f32[40,2,1,128]{3,0,2,1:T(8,128)S(1)}, u32[]{:S(2)}, u32[]{:S(2)}) %collective-permute-start.3) | collective-permute-done | bytes 40992 | tf_op jit(solution)/shard_map/ppermute | solution.py:22
  197.7 3.8 %collective-permute-done.5 = f32[40,2,18,1]{0,2,3,1:T(8,128)S(1)} collective-permute-done((f32[40,2,18,1]{0,2,3,1:T(8,128)S(1)}, f32[40,2,18,1]{0,2,3,1:T(8,128)S(1)}, u32[]{:S(2)}, u32[]{:S(2)}) %collective-permute-start.5) | collective-permute-done | bytes 5792 | tf_op jit(solution)/shard_map/ppermute | solution.py:22
  (259 shorter events, 74.5 us)
Async XLA Ops:
  6.5 4.8 %copy-start.2 = (s32[8192]{0:T(1024)S(1)}, s32[8192]{0:T(1024)}, u32[]{:S(2)}) copy-start(s32[8192]{0:T(1024)} %param.19) | copy-start | bytes 98308
  6.5 4.8 %copy-start.3 = (s32[8192]{0:T(1024)S(1)}, s32[8192]{0:T(1024)}, u32[]{:S(2)}) copy-start(s32[8192]{0:T(1024)} %param.20) | copy-start | bytes 98308
  6.5 4.8 %copy-start.4 = (f32[8192]{0:T(1024)S(1)}, f32[8192]{0:T(1024)}, u32[]{:S(2)}) copy-start(f32[8192]{0:T(1024)} %param.17) | copy-start | bytes 98308
  32.6 16.0 %all-to-all-start = ((s32[1,16,1536]{2,0,1:T(1,128)}), s32[1,16,1536]{2,0,1:T(1,128)S(1)}, u32[]{:S(2)}, u32[]{:S(2)}) async-start(s32[1,16,1536]{2,0,1:T(1,128)} %convert_element_type.35), calls=%async_computation | async-start | bytes 196608 | tf_op jit(solution)/shard_map/all_to_all | solution.py:91
  48.6 14.9 %all-to-all-start.1 = ((f32[3,16,1536]{2,0,1:T(4,128)}), f32[3,16,1536]{2,0,1:T(4,128)S(1)}, u32[]{:S(2)}, u32[]{:S(2)}) async-start(f32[3,16,1536]{2,0,1:T(4,128)} %copy.54), calls=%async_computation.1 | async-start | bytes 786432 | tf_op jit(solution)/shard_map/all_to_all | solution.py:90
  52.1 127.7 %all-reduce.2.cloned.1.call-start = ((), (), s32[]{:S(2)}) async-start(), calls=%async_computation.2 | async-start | bytes 196608 | tf_op jit(solution)/shard_map/psum | solution.py:145
  72.8 3.9 %copy-start = (f32[2048,204]{0,1:T(8,128)S(1)}, f32[2048,204]{0,1:T(8,128)}, u32[]{:S(2)}) copy-start(f32[2048,204]{0,1:T(8,128)} %mul.212) | copy-start | bytes 5013508 | tf_op jit(solution)/shard_map/while
  80.1 3.9 %copy-start = (f32[2048,204]{0,1:T(8,128)S(1)}, f32[2048,204]{0,1:T(8,128)}, u32[]{:S(2)}) copy-start(f32[2048,204]{0,1:T(8,128)} %mul.212) | copy-start | bytes 5013508 | tf_op jit(solution)/shard_map/while
  87.3 3.9 %copy-start = (f32[2048,204]{0,1:T(8,128)S(1)}, f32[2048,204]{0,1:T(8,128)}, u32[]{:S(2)}) copy-start(f32[2048,204]{0,1:T(8,128)} %mul.212) | copy-start | bytes 5013508 | tf_op jit(solution)/shard_map/while
  94.6 3.9 %copy-start = (f32[2048,204]{0,1:T(8,128)S(1)}, f32[2048,204]{0,1:T(8,128)}, u32[]{:S(2)}) copy-start(f32[2048,204]{0,1:T(8,128)} %mul.212) | copy-start | bytes 5013508 | tf_op jit(solution)/shard_map/while
  101.8 3.9 %copy-start = (f32[2048,204]{0,1:T(8,128)S(1)}, f32[2048,204]{0,1:T(8,128)}, u32[]{:S(2)}) copy-start(f32[2048,204]{0,1:T(8,128)} %mul.212) | copy-start | bytes 5013508 | tf_op jit(solution)/shard_map/while
  109.1 3.9 %copy-start = (f32[2048,204]{0,1:T(8,128)S(1)}, f32[2048,204]{0,1:T(8,128)}, u32[]{:S(2)}) copy-start(f32[2048,204]{0,1:T(8,128)} %mul.212) | copy-start | bytes 5013508 | tf_op jit(solution)/shard_map/while
  116.3 3.9 %copy-start = (f32[2048,204]{0,1:T(8,128)S(1)}, f32[2048,204]{0,1:T(8,128)}, u32[]{:S(2)}) copy-start(f32[2048,204]{0,1:T(8,128)} %mul.212) | copy-start | bytes 5013508 | tf_op jit(solution)/shard_map/while
  123.6 3.9 %copy-start = (f32[2048,204]{0,1:T(8,128)S(1)}, f32[2048,204]{0,1:T(8,128)}, u32[]{:S(2)}) copy-start(f32[2048,204]{0,1:T(8,128)} %mul.212) | copy-start | bytes 5013508 | tf_op jit(solution)/shard_map/while
  130.9 3.9 %copy-start = (f32[2048,204]{0,1:T(8,128)S(1)}, f32[2048,204]{0,1:T(8,128)}, u32[]{:S(2)}) copy-start(f32[2048,204]{0,1:T(8,128)} %mul.212) | copy-start | bytes 5013508 | tf_op jit(solution)/shard_map/while
  138.1 3.9 %copy-start = (f32[2048,204]{0,1:T(8,128)S(1)}, f32[2048,204]{0,1:T(8,128)}, u32[]{:S(2)}) copy-start(f32[2048,204]{0,1:T(8,128)} %mul.212) | copy-start | bytes 5013508 | tf_op jit(solution)/shard_map/while
  145.4 3.9 %copy-start = (f32[2048,204]{0,1:T(8,128)S(1)}, f32[2048,204]{0,1:T(8,128)}, u32[]{:S(2)}) copy-start(f32[2048,204]{0,1:T(8,128)} %mul.212) | copy-start | bytes 5013508 | tf_op jit(solution)/shard_map/while
  150.7 29.1 %copy-start.1 = (bf16[40,6,2,16,128]{4,3,2,1,0:T(8,128)(2,1)S(1)}, bf16[40,6,2,16,128]{4,3,2,1,0:T(8,128)(2,1)}, u32[]{:S(2)}) copy-start(bf16[40,6,2,16,128]{4,3,2,1,0:T(8,128)(2,1)} %param.23) | copy-start | bytes 5898244
  150.8 3.9 %collective-permute-start = (f32[12,17]{1,0:T(8,128)S(1)}, f32[12,17]{1,0:T(8,128)S(1)}, u32[]{:S(2)}, u32[]{:S(2)}) collective-permute-start(f32[12,17]{1,0:T(8,128)S(1)} %reshape.290), channel_id=1, source_target_pairs={{0,2},{1,3},{4,6},{5,7},{8,10},{9,11},{12,14},{13,15},{16,18},{17,... | collective-permute-start | bytes 2456 | tf_op jit(solution)/shard_map/ppermute | solution.py:11
  155.5 4.1 %collective-permute-start.1 = (f32[12,128]{1,0:T(8,128)S(1)}, f32[12,128]{1,0:T(8,128)S(1)}, u32[]{:S(2)}, u32[]{:S(2)}) collective-permute-start(f32[12,128]{1,0:T(8,128)S(1)} %scatter-add.11), channel_id=1, source_target_pairs={{0,4},{4,8},{8,12},{12,16},{16,20},{20,24},{24,28},{1,5},{5,9},{9,... | collective-permute-start | bytes 18440 | tf_op jit(solution)/shard_map/ppermute | solution.py:11
  181.3 5.3 %collective-permute-start.2 = (f32[40,2,1,128]{3,0,2,1:T(8,128)S(1)}, f32[40,2,1,128]{3,0,2,1:T(8,128)S(1)}, u32[]{:S(2)}, u32[]{:S(2)}) collective-permute-start(f32[40,2,1,128]{3,0,2,1:T(8,128)S(1)} %copy.61), channel_id=1, source_target_pairs={{0,4},{4,8},{8,12},{12,16},{16,20},{20,24},{24,28},{1,5},{5,9},{9,... | collective-permute-start | bytes 122888 | tf_op jit(solution)/shard_map/ppermute | solution.py:21
  185.0 5.9 %collective-permute-start.3 = (f32[40,2,1,128]{3,0,2,1:T(8,128)S(1)}, f32[40,2,1,128]{3,0,2,1:T(8,128)S(1)}, u32[]{:S(2)}, u32[]{:S(2)}) collective-permute-start(f32[40,2,1,128]{3,0,2,1:T(8,128)S(1)} %copy.62), channel_id=1, source_target_pairs={{4,0},{8,4},{12,8},{16,12},{20,16},{24,20},{28,24},{5,1},{9,5},{13... | collective-permute-start | bytes 122888 | tf_op jit(solution)/shard_map/ppermute | solution.py:22
  191.9 5.4 %collective-permute-start.4 = (f32[40,2,18,1]{0,2,3,1:T(8,128)S(1)}, f32[40,2,18,1]{0,2,3,1:T(8,128)S(1)}, u32[]{:S(2)}, u32[]{:S(2)}) collective-permute-start(f32[40,2,18,1]{0,2,3,1:T(8,128)S(1)} %copy.65), channel_id=1, source_target_pairs={{0,2},{1,3},{4,6},{5,7},{8,10},{9,11},{12,14},{13,15},{16,18},{17,... | collective-permute-start | bytes 17288 | tf_op jit(solution)/shard_map/ppermute | solution.py:21
  195.8 5.7 %collective-permute-start.5 = (f32[40,2,18,1]{0,2,3,1:T(8,128)S(1)}, f32[40,2,18,1]{0,2,3,1:T(8,128)S(1)}, u32[]{:S(2)}, u32[]{:S(2)}) collective-permute-start(f32[40,2,18,1]{0,2,3,1:T(8,128)S(1)} %copy.66), channel_id=1, source_target_pairs={{2,0},{3,1},{6,4},{7,5},{10,8},{11,9},{14,12},{15,13},{18,16},{19,... | collective-permute-start | bytes 17288 | tf_op jit(solution)/shard_map/ppermute | solution.py:22
  (1 other events, 3.9 us)
Sparse Core Ops, SparseCore 0:
  160.5 19.3 all-reduce.1
where the time goes:
time: 211 us
  matrix products  84.9 us (40%)
  waiting for transfers between devices  47.1 us (22%)
  starting transfers between devices  26.9 us (13%)
  local copies, waits for them, and re-layouts  24.9 us (12%)
  between operations  14.4 us (7%)
  other arithmetic  11 us (5%)
    dot_general x28, matrix products, contract_rows(): lax.dot_general(left, right, (((0,), (0,)), ((), ())), precision=lax.Prec...  83.7 us
    psum x1, waiting for transfers between devices, body(): grad = lax.psum(interior, 'mem')  19.5 us
    mul x12, local copies, waits for them, and re-layouts, spread_rows(): layer_hot[:, :, None] * weight_x[:, None, :]  17.2 us
    all_to_all x1, waiting for transfers between devices, body(): lax.all_to_all(send_floats, ('tx', 'ty'), split_axis=1, concat_axis=1, ti...  11.2 us
    all_to_all x1, starting transfers between devices, body(): lax.all_to_all(send_index, ('tx', 'ty'), split_axis=1, concat_axis=1, til...  8.34 us
    ppermute x2, waiting for transfers between devices, extended_2(): after = lax.ppermute(initial, axis, down)  8.04 us
    ppermute x2, starting transfers between devices, extended_2(): before = lax.ppermute(last, axis, up)  7.05 us
    all_to_all x1, waiting for transfers between devices, body(): lax.all_to_all(send_index, ('tx', 'ty'), split_axis=1, concat_axis=1, til...  6.68 us
  transfers between devices with their start and end apart: 9, of which 8 were waited for; matrix products, arithmetic and copies ran while one was open for 2% of the time, Pallas kernels for 0%

commit v1 on v0

--- a/solution.py
+++ b/solution.py
@@ -142,7 +142,11 @@
     east_rim = east_rim.at[:, 0].add(from_south[:, cells_x])
     from_west = shifted(east_rim, "tx", 1)
     interior = interior.at[:, 0, :].add(from_west)
-    grad = lax.psum(interior, "mem")
+
+    def yards_cover(original, mesh_ax):
+        return jnp.sum(lax.all_gather(original, mesh_ax), axis=0)
+
+    grad = yards_cover(interior, "mem")
     grad_slots = grad.reshape(slot_count, level_count, cells_x, cells_y)
     contrib = jnp.sum(ensemble * grad_slots[None], axis=1)
     padded = extended_2(contrib, (("tx", 2), ("ty", 3)), 1)

time: 211 us -> 181 us (0.86)
  waiting for transfers between devices: 47.1 us -> 28.3 us
  between operations: 14.4 us -> 1.06 us
  blocking collectives: 0 us -> 2.13 us
    psum x1 -> x0, waiting for transfers between devices: 19.5 us -> none  [body(): grad = lax.psum(interior, 'mem')]
    all_gather x0 -> x1, blocking collectives: none -> 2.13 us  [yards_cover(): return jnp.sum(lax.all_gather(original, mesh_ax), axis=0)]
  transfers between devices with their start and end apart: 9 -> 8, of which waited for: 8 -> 7; matrix products, arithmetic and copies ran while one was open for 2% -> 2% of each run, Pallas kernels for 0% -> 0%
where the time goes in v1:
time: 181 us; the launch traced here: 180 us
  matrix products  84.9 us (47%)
  waiting for transfers between devices  28.3 us (16%)
  starting transfers between devices  28.2 us (16%)
  local copies, waits for them, and re-layouts  24.1 us (13%)
  other arithmetic  10.1 us (6%)
  blocking collectives  2.13 us (1%)
    dot_general x28, matrix products, contract_rows(): lax.dot_general(left, right, (((0,), (0,)), ((), ())), precision=lax.Prec...  83.7 us
    mul x12, local copies, waits for them, and re-layouts, spread_rows(): layer_hot[:, :, None] * weight_x[:, None, :]  17.1 us
    all_to_all x1, waiting for transfers between devices, body(): lax.all_to_all(send_floats, ('tx', 'ty'), split_axis=1, concat_axis=1, ti...  11.2 us
    ppermute x2, waiting for transfers between devices, extended_2(): after = lax.ppermute(initial, axis, down)  8.62 us
    ppermute x2, starting transfers between devices, extended_2(): before = lax.ppermute(last, axis, up)  8.37 us
    all_to_all x1, starting transfers between devices, body(): lax.all_to_all(send_index, ('tx', 'ty'), split_axis=1, concat_axis=1, til...  8.36 us
    all_to_all x1, waiting for transfers between devices, body(): lax.all_to_all(send_index, ('tx', 'ty'), split_axis=1, concat_axis=1, til...  6.65 us
    ppermute x2, starting transfers between devices, shifted(): return lax.ppermute(block, axis, route)  5.36 us
  transfers between devices with their start and end apart: 8, of which 7 were waited for; matrix products, arithmetic and copies ran while one was open for 2% of the time, Pallas kernels for 0%

profile of v1, /device:TPU:0, one launch (start us, length us, event | category | flops | bytes accessed | tf_op | source)
XLA Modules:
  0.0 180.2 jit_solution(8685337742207349537)
XLA Ops:
  5.0 20.3 %while.34 = (s32[]{:T(128)}, f32[64,1536]{1,0:T(8,128)S(1)}, f32[8192,4]{0,1:T(4,128)S(1)}, f32[8192,16]{0,1:T(8,128)S(1)}, s32[8192]{0:T(1024)S(1)}, /*index=5*/s32[]{:T(128)}, s32[]{:T(128)}, s32[]{:T(128)}, s32[]{:T(128)}) while((s32[]{:T(128)}, f32[64,1536]{1,0:T(8,128)S(1)}, f32[8192,4]{0,1:T(4,128)S(1)}, ...), condition=%wide.region_4.5_spmd.clone, body=%wide.region_3.4_spmd.clone.sunk | while | flops 2419392512 | bytes 2351265 | solution.py:83
  5.1 4.9 %fusion.60 = f32[64,1536]{1,0:T(8,128)S(1)} fusion(f32[2048,64]{0,1:T(8,128)S(1)} %bitcast.64, s32[2048]{0:T(1024)S(1)} %dynamic_slice.94, f32[64,1536]{1,0:T(8,128)S(1)} %get-tuple-element.605, pred[]{:T(512)S(6)} %compare.33), kind=kOutput, calls=%fused_computation.7.clone.1 | convolution fusion | flops 2419261440 | bytes 1318913 | tf_op jit(solution)/shard_map/while/body/eval_jaxpr/dot_general | solution.py:33
  10.2 4.9 %fusion.60 = f32[64,1536]{1,0:T(8,128)S(1)} fusion(f32[2048,64]{0,1:T(8,128)S(1)} %bitcast.64, s32[2048]{0:T(1024)S(1)} %dynamic_slice.94, f32[64,1536]{1,0:T(8,128)S(1)} %get-tuple-element.605, pred[]{:T(512)S(6)} %compare.33), kind=kOutput, calls=%fused_computation.7.clone.1 | convolution fusion | flops 2419261440 | bytes 1318913 | tf_op jit(solution)/shard_map/while/body/eval_jaxpr/dot_general | solution.py:33
  15.3 4.9 %fusion.60 = f32[64,1536]{1,0:T(8,128)S(1)} fusion(f32[2048,64]{0,1:T(8,128)S(1)} %bitcast.64, s32[2048]{0:T(1024)S(1)} %dynamic_slice.94, f32[64,1536]{1,0:T(8,128)S(1)} %get-tuple-element.605, pred[]{:T(512)S(6)} %compare.33), kind=kOutput, calls=%fused_computation.7.clone.1 | convolution fusion | flops 2419261440 | bytes 1318913 | tf_op jit(solution)/shard_map/while/body/eval_jaxpr/dot_general | solution.py:33
  20.4 4.9 %fusion.60 = f32[64,1536]{1,0:T(8,128)S(1)} fusion(f32[2048,64]{0,1:T(8,128)S(1)} %bitcast.64, s32[2048]{0:T(1024)S(1)} %dynamic_slice.94, f32[64,1536]{1,0:T(8,128)S(1)} %get-tuple-element.605, pred[]{:T(512)S(6)} %compare.33), kind=kOutput, calls=%fused_computation.7.clone.1 | convolution fusion | flops 2419261440 | bytes 1318913 | tf_op jit(solution)/shard_map/while/body/eval_jaxpr/dot_general | solution.py:33
  26.0 8.4 %all-to-all-start = ((s32[1,16,1536]{2,0,1:T(1,128)}), s32[1,16,1536]{2,0,1:T(1,128)S(1)}, u32[]{:S(2)}, u32[]{:S(2)}) async-start(s32[1,16,1536]{2,0,1:T(1,128)} %convert_element_type.35), calls=%async_computation | async-start | bytes 196608 | tf_op jit(solution)/shard_map/all_to_all | solution.py:91
  35.4 6.7 %all-to-all-done = s32[1,16,1536]{2,0,1:T(1,128)S(1)} async-done(((s32[1,16,1536]{2,0,1:T(1,128)}), s32[1,16,1536]{2,0,1:T(1,128)S(1)}, u32[]{:S(2)}, u32[]{:S(2)}) %all-to-all-start) | async-done | bytes 98336 | tf_op jit(solution)/shard_map/all_to_all | solution.py:91
  45.8 11.2 %all-to-all-done.1 = f32[3,16,1536]{2,0,1:T(4,128)S(1)} async-done(((f32[3,16,1536]{2,0,1:T(4,128)}), f32[3,16,1536]{2,0,1:T(4,128)S(1)}, u32[]{:S(2)}, u32[]{:S(2)}) %all-to-all-start.1) | async-done | bytes 294944 | tf_op jit(solution)/shard_map/all_to_all | solution.py:90
  57.2 86.9 %while.35 = (s32[]{:T(128)}, f32[204,128]{1,0:T(8,128)S(1)}, f32[204]{0:T(256)S(1)}, s32[24576]{0:T(1024)S(1)}, f32[24576]{0:T(1024)S(1)}, /*index=5*/s32[24576]...) while((s32[]{:T(128)}, f32[204,128]{1,0:T(8,128)S(1)}, ...), condition=%wide.region_6.7_spmd.clone.clone, body=%wide.region_5.6_spmd.clone.clone.sunk | while | flops 648760704 | bytes 15973794 | solution.py:135
  59.1 3.9 %convolution_add_fusion.3 = f32[204,128]{1,0:T(8,128)S(1)} fusion(f32[2048,204]{0,1:T(8,128)} %mul.212, f32[2048]{0:T(1024)S(1)} %get-tuple-element.592, s32[2048]{0:T(1024)S(1)} %broadcast_add_fusion.5, f32[2048]{0:T(1024)S(1)} %broadcast_subtract_fusion.3, s32[2048]{0:T(1024)S(1)} %get-tuple-element.593, f32[204,128]{1,0:T(8,128)S(1)} %get-tuple-element.636, ...), kind=kOutput, calls=%fused_computation.14.clone.1 | convolution fusion | flops 643091456 | bytes 1912833 | tf_op jit(solution)/shard_map/while/body/eval_jaxpr/dot_general | solution.py:33
  66.3 3.9 %convolution_add_fusion.3 = f32[204,128]{1,0:T(8,128)S(1)} fusion(f32[2048,204]{0,1:T(8,128)} %mul.212, f32[2048]{0:T(1024)S(1)} %get-tuple-element.592, s32[2048]{0:T(1024)S(1)} %broadcast_add_fusion.5, f32[2048]{0:T(1024)S(1)} %broadcast_subtract_fusion.3, s32[2048]{0:T(1024)S(1)} %get-tuple-element.593, f32[204,128]{1,0:T(8,128)S(1)} %get-tuple-element.636, ...), kind=kOutput, calls=%fused_computation.14.clone.1 | convolution fusion | flops 643091456 | bytes 1912833 | tf_op jit(solution)/shard_map/while/body/eval_jaxpr/dot_general | solution.py:33
  73.6 3.9 %convolution_add_fusion.3 = f32[204,128]{1,0:T(8,128)S(1)} fusion(f32[2048,204]{0,1:T(8,128)} %mul.212, f32[2048]{0:T(1024)S(1)} %get-tuple-element.592, s32[2048]{0:T(1024)S(1)} %broadcast_add_fusion.5, f32[2048]{0:T(1024)S(1)} %broadcast_subtract_fusion.3, s32[2048]{0:T(1024)S(1)} %get-tuple-element.593, f32[204,128]{1,0:T(8,128)S(1)} %get-tuple-element.636, ...), kind=kOutput, calls=%fused_computation.14.clone.1 | convolution fusion | flops 643091456 | bytes 1912833 | tf_op jit(solution)/shard_map/while/body/eval_jaxpr/dot_general | solution.py:33
  80.8 3.9 %convolution_add_fusion.3 = f32[204,128]{1,0:T(8,128)S(1)} fusion(f32[2048,204]{0,1:T(8,128)} %mul.212, f32[2048]{0:T(1024)S(1)} %get-tuple-element.592, s32[2048]{0:T(1024)S(1)} %broadcast_add_fusion.5, f32[2048]{0:T(1024)S(1)} %broadcast_subtract_fusion.3, s32[2048]{0:T(1024)S(1)} %get-tuple-element.593, f32[204,128]{1,0:T(8,128)S(1)} %get-tuple-element.636, ...), kind=kOutput, calls=%fused_computation.14.clone.1 | convolution fusion | flops 643091456 | bytes 1912833 | tf_op jit(solution)/shard_map/while/body/eval_jaxpr/dot_general | solution.py:33
  88.0 3.9 %convolution_add_fusion.3 = f32[204,128]{1,0:T(8,128)S(1)} fusion(f32[2048,204]{0,1:T(8,128)} %mul.212, f32[2048]{0:T(1024)S(1)} %get-tuple-element.592, s32[2048]{0:T(1024)S(1)} %broadcast_add_fusion.5, f32[2048]{0:T(1024)S(1)} %broadcast_subtract_fusion.3, s32[2048]{0:T(1024)S(1)} %get-tuple-element.593, f32[204,128]{1,0:T(8,128)S(1)} %get-tuple-element.636, ...), kind=kOutput, calls=%fused_computation.14.clone.1 | convolution fusion | flops 643091456 | bytes 1912833 | tf_op jit(solution)/shard_map/while/body/eval_jaxpr/dot_general | solution.py:33
  95.3 3.9 %convolution_add_fusion.3 = f32[204,128]{1,0:T(8,128)S(1)} fusion(f32[2048,204]{0,1:T(8,128)} %mul.212, f32[2048]{0:T(1024)S(1)} %get-tuple-element.592, s32[2048]{0:T(1024)S(1)} %broadcast_add_fusion.5, f32[2048]{0:T(1024)S(1)} %broadcast_subtract_fusion.3, s32[2048]{0:T(1024)S(1)} %get-tuple-element.593, f32[204,128]{1,0:T(8,128)S(1)} %get-tuple-element.636, ...), kind=kOutput, calls=%fused_computation.14.clone.1 | convolution fusion | flops 643091456 | bytes 1912833 | tf_op jit(solution)/shard_map/while/body/eval_jaxpr/dot_general | solution.py:33
  102.5 3.9 %convolution_add_fusion.3 = f32[204,128]{1,0:T(8,128)S(1)} fusion(f32[2048,204]{0,1:T(8,128)} %mul.212, f32[2048]{0:T(1024)S(1)} %get-tuple-element.592, s32[2048]{0:T(1024)S(1)} %broadcast_add_fusion.5, f32[2048]{0:T(1024)S(1)} %broadcast_subtract_fusion.3, s32[2048]{0:T(1024)S(1)} %get-tuple-element.593, f32[204,128]{1,0:T(8,128)S(1)} %get-tuple-element.636, ...), kind=kOutput, calls=%fused_computation.14.clone.1 | convolution fusion | flops 643091456 | bytes 1912833 | tf_op jit(solution)/shard_map/while/body/eval_jaxpr/dot_general | solution.py:33
  109.8 3.9 %convolution_add_fusion.3 = f32[204,128]{1,0:T(8,128)S(1)} fusion(f32[2048,204]{0,1:T(8,128)} %mul.212, f32[2048]{0:T(1024)S(1)} %get-tuple-element.592, s32[2048]{0:T(1024)S(1)} %broadcast_add_fusion.5, f32[2048]{0:T(1024)S(1)} %broadcast_subtract_fusion.3, s32[2048]{0:T(1024)S(1)} %get-tuple-element.593, f32[204,128]{1,0:T(8,128)S(1)} %get-tuple-element.636, ...), kind=kOutput, calls=%fused_computation.14.clone.1 | convolution fusion | flops 643091456 | bytes 1912833 | tf_op jit(solution)/shard_map/while/body/eval_jaxpr/dot_general | solution.py:33
  117.0 3.9 %convolution_add_fusion.3 = f32[204,128]{1,0:T(8,128)S(1)} fusion(f32[2048,204]{0,1:T(8,128)} %mul.212, f32[2048]{0:T(1024)S(1)} %get-tuple-element.592, s32[2048]{0:T(1024)S(1)} %broadcast_add_fusion.5, f32[2048]{0:T(1024)S(1)} %broadcast_subtract_fusion.3, s32[2048]{0:T(1024)S(1)} %get-tuple-element.593, f32[204,128]{1,0:T(8,128)S(1)} %get-tuple-element.636, ...), kind=kOutput, calls=%fused_computation.14.clone.1 | convolution fusion | flops 643091456 | bytes 1912833 | tf_op jit(solution)/shard_map/while/body/eval_jaxpr/dot_general | solution.py:33
  124.3 3.9 %convolution_add_fusion.3 = f32[204,128]{1,0:T(8,128)S(1)} fusion(f32[2048,204]{0,1:T(8,128)} %mul.212, f32[2048]{0:T(1024)S(1)} %get-tuple-element.592, s32[2048]{0:T(1024)S(1)} %broadcast_add_fusion.5, f32[2048]{0:T(1024)S(1)} %broadcast_subtract_fusion.3, s32[2048]{0:T(1024)S(1)} %get-tuple-element.593, f32[204,128]{1,0:T(8,128)S(1)} %get-tuple-element.636, ...), kind=kOutput, calls=%fused_computation.14.clone.1 | convolution fusion | flops 643091456 | bytes 1912833 | tf_op jit(solution)/shard_map/while/body/eval_jaxpr/dot_general | solution.py:33
  131.5 3.9 %convolution_add_fusion.3 = f32[204,128]{1,0:T(8,128)S(1)} fusion(f32[2048,204]{0,1:T(8,128)} %mul.212, f32[2048]{0:T(1024)S(1)} %get-tuple-element.592, s32[2048]{0:T(1024)S(1)} %broadcast_add_fusion.5, f32[2048]{0:T(1024)S(1)} %broadcast_subtract_fusion.3, s32[2048]{0:T(1024)S(1)} %get-tuple-element.593, f32[204,128]{1,0:T(8,128)S(1)} %get-tuple-element.636, ...), kind=kOutput, calls=%fused_computation.14.clone.1 | convolution fusion | flops 643091456 | bytes 1912833 | tf_op jit(solution)/shard_map/while/body/eval_jaxpr/dot_general | solution.py:33
  138.7 3.9 %convolution_add_fusion.3 = f32[204,128]{1,0:T(8,128)S(1)} fusion(f32[2048,204]{0,1:T(8,128)} %mul.212, f32[2048]{0:T(1024)S(1)} %get-tuple-element.592, s32[2048]{0:T(1024)S(1)} %broadcast_add_fusion.5, f32[2048]{0:T(1024)S(1)} %broadcast_subtract_fusion.3, s32[2048]{0:T(1024)S(1)} %get-tuple-element.593, f32[204,128]{1,0:T(8,128)S(1)} %get-tuple-element.636, ...), kind=kOutput, calls=%fused_computation.14.clone.1 | convolution fusion | flops 643091456 | bytes 1912833 | tf_op jit(solution)/shard_map/while/body/eval_jaxpr/dot_general | solution.py:33
  155.8 4.2 %collective-permute-start.2 = (f32[40,2,1,128]{3,0,2,1:T(8,128)S(1)}, f32[40,2,1,128]{3,0,2,1:T(8,128)S(1)}, u32[]{:S(2)}, u32[]{:S(2)}) collective-permute-start(f32[40,2,1,128]{3,0,2,1:T(8,128)S(1)} %copy.66), channel_id=1, source_target_pairs={{0,4},{4,8},{8,12},{12,16},{16,20},{20,24},{24,28},{1,5},{5,9},{9,... | collective-permute-start | bytes 122888 | tf_op jit(solution)/shard_map/ppermute | solution.py:21
  161.7 4.8 %collective-permute-done.3 = f32[40,2,1,128]{3,0,2,1:T(8,128)S(1)} collective-permute-done((f32[40,2,1,128]{3,0,2,1:T(8,128)S(1)}, f32[40,2,1,128]{3,0,2,1:T(8,128)S(1)}, u32[]{:S(2)}, u32[]{:S(2)}) %collective-permute-start.3) | collective-permute-done | bytes 40992 | tf_op jit(solution)/shard_map/ppermute | solution.py:22
  167.5 4.2 %collective-permute-start.4 = (f32[40,2,18,1]{0,2,3,1:T(8,128)S(1)}, f32[40,2,18,1]{0,2,3,1:T(8,128)S(1)}, u32[]{:S(2)}, u32[]{:S(2)}) collective-permute-start(f32[40,2,18,1]{0,2,3,1:T(8,128)S(1)} %copy.70), channel_id=1, source_target_pairs={{0,2},{1,3},{4,6},{5,7},{8,10},{9,11},{12,14},{13,15},{16,18},{17,... | collective-permute-start | bytes 17288 | tf_op jit(solution)/shard_map/ppermute | solution.py:21
  (259 shorter events, 71.6 us)
Async XLA Ops:
  0.0 4.8 %copy-start.2 = (s32[8192]{0:T(1024)S(1)}, s32[8192]{0:T(1024)}, u32[]{:S(2)}) copy-start(s32[8192]{0:T(1024)} %param.19) | copy-start | bytes 98308
  0.0 4.8 %copy-start.3 = (s32[8192]{0:T(1024)S(1)}, s32[8192]{0:T(1024)}, u32[]{:S(2)}) copy-start(s32[8192]{0:T(1024)} %param.20) | copy-start | bytes 98308
  0.0 4.8 %copy-start.4 = (f32[8192]{0:T(1024)S(1)}, f32[8192]{0:T(1024)}, u32[]{:S(2)}) copy-start(f32[8192]{0:T(1024)} %param.17) | copy-start | bytes 98308
  26.0 16.0 %all-to-all-start = ((s32[1,16,1536]{2,0,1:T(1,128)}), s32[1,16,1536]{2,0,1:T(1,128)S(1)}, u32[]{:S(2)}, u32[]{:S(2)}) async-start(s32[1,16,1536]{2,0,1:T(1,128)} %convert_element_type.35), calls=%async_computation | async-start | bytes 196608 | tf_op jit(solution)/shard_map/all_to_all | solution.py:91
  42.1 14.9 %all-to-all-start.1 = ((f32[3,16,1536]{2,0,1:T(4,128)}), f32[3,16,1536]{2,0,1:T(4,128)S(1)}, u32[]{:S(2)}, u32[]{:S(2)}) async-start(f32[3,16,1536]{2,0,1:T(4,128)} %copy.57), calls=%async_computation.1 | async-start | bytes 786432 | tf_op jit(solution)/shard_map/all_to_all | solution.py:90
  59.1 3.9 %copy-start = (f32[2048,204]{0,1:T(8,128)S(1)}, f32[2048,204]{0,1:T(8,128)}, u32[]{:S(2)}) copy-start(f32[2048,204]{0,1:T(8,128)} %mul.212) | copy-start | bytes 5013508 | tf_op jit(solution)/shard_map/while
  66.3 3.9 %copy-start = (f32[2048,204]{0,1:T(8,128)S(1)}, f32[2048,204]{0,1:T(8,128)}, u32[]{:S(2)}) copy-start(f32[2048,204]{0,1:T(8,128)} %mul.212) | copy-start | bytes 5013508 | tf_op jit(solution)/shard_map/while
  73.6 3.9 %copy-start = (f32[2048,204]{0,1:T(8,128)S(1)}, f32[2048,204]{0,1:T(8,128)}, u32[]{:S(2)}) copy-start(f32[2048,204]{0,1:T(8,128)} %mul.212) | copy-start | bytes 5013508 | tf_op jit(solution)/shard_map/while
  80.8 3.9 %copy-start = (f32[2048,204]{0,1:T(8,128)S(1)}, f32[2048,204]{0,1:T(8,128)}, u32[]{:S(2)}) copy-start(f32[2048,204]{0,1:T(8,128)} %mul.212) | copy-start | bytes 5013508 | tf_op jit(solution)/shard_map/while
  88.0 3.9 %copy-start = (f32[2048,204]{0,1:T(8,128)S(1)}, f32[2048,204]{0,1:T(8,128)}, u32[]{:S(2)}) copy-start(f32[2048,204]{0,1:T(8,128)} %mul.212) | copy-start | bytes 5013508 | tf_op jit(solution)/shard_map/while
  95.3 3.9 %copy-start = (f32[2048,204]{0,1:T(8,128)S(1)}, f32[2048,204]{0,1:T(8,128)}, u32[]{:S(2)}) copy-start(f32[2048,204]{0,1:T(8,128)} %mul.212) | copy-start | bytes 5013508 | tf_op jit(solution)/shard_map/while
  102.5 3.9 %copy-start = (f32[2048,204]{0,1:T(8,128)S(1)}, f32[2048,204]{0,1:T(8,128)}, u32[]{:S(2)}) copy-start(f32[2048,204]{0,1:T(8,128)} %mul.212) | copy-start | bytes 5013508 | tf_op jit(solution)/shard_map/while
  109.8 3.9 %copy-start = (f32[2048,204]{0,1:T(8,128)S(1)}, f32[2048,204]{0,1:T(8,128)}, u32[]{:S(2)}) copy-start(f32[2048,204]{0,1:T(8,128)} %mul.212) | copy-start | bytes 5013508 | tf_op jit(solution)/shard_map/while
  117.0 3.9 %copy-start = (f32[2048,204]{0,1:T(8,128)S(1)}, f32[2048,204]{0,1:T(8,128)}, u32[]{:S(2)}) copy-start(f32[2048,204]{0,1:T(8,128)} %mul.212) | copy-start | bytes 5013508 | tf_op jit(solution)/shard_map/while
  124.3 3.9 %copy-start = (f32[2048,204]{0,1:T(8,128)S(1)}, f32[2048,204]{0,1:T(8,128)}, u32[]{:S(2)}) copy-start(f32[2048,204]{0,1:T(8,128)} %mul.212) | copy-start | bytes 5013508 | tf_op jit(solution)/shard_map/while
  131.5 3.9 %copy-start = (f32[2048,204]{0,1:T(8,128)S(1)}, f32[2048,204]{0,1:T(8,128)}, u32[]{:S(2)}) copy-start(f32[2048,204]{0,1:T(8,128)} %mul.212) | copy-start | bytes 5013508 | tf_op jit(solution)/shard_map/while
  138.7 3.9 %copy-start = (f32[2048,204]{0,1:T(8,128)S(1)}, f32[2048,204]{0,1:T(8,128)}, u32[]{:S(2)}) copy-start(f32[2048,204]{0,1:T(8,128)} %mul.212) | copy-start | bytes 5013508 | tf_op jit(solution)/shard_map/while
  144.1 11.1 %copy-start.1 = (bf16[40,6,2,16,128]{4,3,2,1,0:T(8,128)(2,1)S(1)}, bf16[40,6,2,16,128]{4,3,2,1,0:T(8,128)(2,1)}, u32[]{:S(2)}) copy-start(bf16[40,6,2,16,128]{4,3,2,1,0:T(8,128)(2,1)} %param.23) | copy-start | bytes 5898244
  144.2 4.0 %collective-permute-start = (f32[12,17]{1,0:T(8,128)S(1)}, f32[12,17]{1,0:T(8,128)S(1)}, u32[]{:S(2)}, u32[]{:S(2)}) collective-permute-start(f32[12,17]{1,0:T(8,128)S(1)} %reshape.292), channel_id=1, source_target_pairs={{0,2},{1,3},{4,6},{5,7},{8,10},{9,11},{12,14},{13,15},{16,18},{17,... | collective-permute-start | bytes 2456 | tf_op jit(solution)/shard_map/ppermute | solution.py:11
  148.9 4.1 %collective-permute-start.1 = (f32[12,128]{1,0:T(8,128)S(1)}, f32[12,128]{1,0:T(8,128)S(1)}, u32[]{:S(2)}, u32[]{:S(2)}) collective-permute-start(f32[12,128]{1,0:T(8,128)S(1)} %scatter-add.11), channel_id=1, source_target_pairs={{0,4},{4,8},{8,12},{12,16},{16,20},{20,24},{24,28},{1,5},{5,9},{9,... | collective-permute-start | bytes 18440 | tf_op jit(solution)/shard_map/ppermute | solution.py:11
  155.8 5.9 %collective-permute-start.2 = (f32[40,2,1,128]{3,0,2,1:T(8,128)S(1)}, f32[40,2,1,128]{3,0,2,1:T(8,128)S(1)}, u32[]{:S(2)}, u32[]{:S(2)}) collective-permute-start(f32[40,2,1,128]{3,0,2,1:T(8,128)S(1)} %copy.66), channel_id=1, source_target_pairs={{0,4},{4,8},{8,12},{12,16},{16,20},{20,24},{24,28},{1,5},{5,9},{9,... | collective-permute-start | bytes 122888 | tf_op jit(solution)/shard_map/ppermute | solution.py:21
  160.0 6.5 %collective-permute-start.3 = (f32[40,2,1,128]{3,0,2,1:T(8,128)S(1)}, f32[40,2,1,128]{3,0,2,1:T(8,128)S(1)}, u32[]{:S(2)}, u32[]{:S(2)}) collective-permute-start(f32[40,2,1,128]{3,0,2,1:T(8,128)S(1)} %copy.67), channel_id=1, source_target_pairs={{4,0},{8,4},{12,8},{16,12},{20,16},{24,20},{28,24},{5,1},{9,5},{13... | collective-permute-start | bytes 122888 | tf_op jit(solution)/shard_map/ppermute | solution.py:22
  167.5 6.2 %collective-permute-start.4 = (f32[40,2,18,1]{0,2,3,1:T(8,128)S(1)}, f32[40,2,18,1]{0,2,3,1:T(8,128)S(1)}, u32[]{:S(2)}, u32[]{:S(2)}) collective-permute-start(f32[40,2,18,1]{0,2,3,1:T(8,128)S(1)} %copy.70), channel_id=1, source_target_pairs={{0,2},{1,3},{4,6},{5,7},{8,10},{9,11},{12,14},{13,15},{16,18},{17,... | collective-permute-start | bytes 17288 | tf_op jit(solution)/shard_map/ppermute | solution.py:21
  172.1 5.7 %collective-permute-start.5 = (f32[40,2,18,1]{0,2,3,1:T(8,128)S(1)}, f32[40,2,18,1]{0,2,3,1:T(8,128)S(1)}, u32[]{:S(2)}, u32[]{:S(2)}) collective-permute-start(f32[40,2,18,1]{0,2,3,1:T(8,128)S(1)} %copy.71), channel_id=1, source_target_pairs={{2,0},{3,1},{6,4},{7,5},{10,8},{11,9},{14,12},{15,13},{18,16},{19,... | collective-permute-start | bytes 17288 | tf_op jit(solution)/shard_map/ppermute | solution.py:22
